TPU v7x, 32 devices: a whole 2x2x4 slice. The times are simulated.
32 devices in a mesh: dp: 2 (over x), expert: 4 (over y, core), mp: 4 (over z).
Axes of the slice: x: 2, y: 2, z: 4, core: 2. Of those that a mesh axis runs over, the one named last changes fastest.
Arguments:
- tokens: bfloat16 [1024, 2048], P(('dp', 'expert'), 'mp'), parts along dimension 0, may hold values from -6 to 6
- routes: int32 [1024, 2], P(('dp', 'expert')), parts along dimension 0, may hold values from 0 to 3, all different within a row; in each aligned block of 128 rows (0 to 127, 128 to 255, ...) at most 96 rows name the same one
- gate_num: int32 [1024], P(('dp', 'expert')), parts along dimension 0, may hold values from 1 to 63
- capacity: int32 [4], replicated, may hold values from 48 to 96
- w_up: bfloat16 [2048, 28672], P(None, ('expert', 'mp')), may hold values from -0.125 to 0.125
- w_down: bfloat16 [28672, 2048], P(('expert', 'mp')), may hold values from -0.0625 to 0.0625
Outputs:
- mixed: bfloat16 [1024, 2048], P(('dp', 'expert'), 'mp'), parts along dimension 0
There are 2 independent parts, one for each index of `dp`. A program takes and returns all parts, laid end to end along the dimension named above; an argument that names none is the same for every part. Nothing has to cross between parts.
Inputs may be any that keep to these rules, and one draw needn't show every extreme that they name: `routes`: each row names two different experts; in each aligned block of 128 rows no expert is named by more than 96 rows, a bound that some block reaches.
All inputs are finite; a program needn't handle non-finite values.
Results may differ from a plain program's by a relative error of at most 0.0085.
Values may be sent and summed in bfloat16 or wider, within the bound.
A program may use at most 64 MiB of HBM per device.

v0:
```python
import jax
import jax.numpy as jnp
from jax import lax
from jax.sharding import PartitionSpec as P


def per_device(tokens, routes, gate_num, capacity, w_up, w_down):
    token_count = routes.shape[0]
    expert_count = capacity.shape[0]
    group_size = lax.axis_size("expert") // expert_count
    slot_count = min(token_count, 3 * token_count // expert_count)
    feature_width = w_up.shape[0]
    expert_ids = jnp.arange(expert_count, dtype=jnp.int32)
    matches = routes[:, :, None] == expert_ids[None, None, :]
    named_count = matches.sum(axis=1).astype(jnp.float32)
    token_ids = jnp.arange(token_count, dtype=jnp.int32)
    lower_mask = (token_ids[:, None] > token_ids[None, :]).astype(jnp.float32)
    positions = jnp.dot(
        lower_mask, named_count, precision=lax.Precision.HIGHEST, preferred_element_type=jnp.float32
    ).astype(jnp.int32)
    route_pos = jnp.sum(jnp.where(matches, positions[:, None, :], 0), axis=2)
    route_cap = jnp.sum(jnp.where(matches, capacity[None, None, :], 0), axis=2)
    kept_mask = route_pos < route_cap
    slot_index = jnp.where(kept_mask, routes * slot_count + route_pos, -1)
    first_share = gate_num.astype(jnp.float32) / 64.0
    weights = jnp.where(kept_mask, jnp.stack([first_share, 1.0 - first_share], axis=1), 0.0)
    slot_ids = jnp.arange(expert_count * slot_count, dtype=jnp.int32)
    dispatch_matrix = jnp.any(slot_ids[:, None, None] == slot_index[None, :, :], axis=2).astype(
        jnp.bfloat16
    )
    combine_hits = slot_ids[None, :, None] == slot_index[:, None, :]
    combine_matrix = jnp.sum(jnp.where(combine_hits, weights[:, None, :], 0.0), axis=2)
    whole = lax.all_gather(tokens, "mp", axis=1, tiled=True)
    buffer = jnp.dot(dispatch_matrix, whole, preferred_element_type=jnp.float32).astype(
        jnp.bfloat16
    )
    width = buffer.shape[1]
    grouped = buffer.reshape(expert_count, 1, slot_count, width)
    copies = jnp.broadcast_to(grouped, (expert_count, group_size, slot_count, width))
    received = lax.all_to_all(
        copies.reshape(expert_count * group_size, slot_count, width),
        "expert",
        split_axis=0,
        concat_axis=0,
        tiled=True,
    )
    source_count, count_here, width = received.shape
    flat_rows = received.reshape(source_count * count_here, width)
    hidden = jax.nn.silu(jnp.dot(flat_rows, w_up, preferred_element_type=jnp.float32)).astype(
        jnp.bfloat16
    )
    partial_value = jnp.dot(hidden, w_down, preferred_element_type=jnp.float32).astype(jnp.bfloat16)
    answered = lax.all_to_all(
        partial_value.reshape(source_count, count_here, width),
        "expert",
        split_axis=0,
        concat_axis=0,
        tiled=True,
    )
    summed = (
        answered.astype(jnp.float32)
        .reshape(expert_count, group_size, slot_count, feature_width)
        .sum(axis=1)
    )
    summed = summed.reshape(expert_count * slot_count, feature_width)
    mixed = jnp.dot(
        combine_matrix, summed, precision=lax.Precision.HIGHEST, preferred_element_type=jnp.float32
    )
    return lax.psum_scatter(mixed, "mp", scatter_dimension=1, tiled=True).astype(jnp.bfloat16)


def solution(mesh):
    return jax.shard_map(
        per_device,
        mesh=mesh,
        in_specs=(
            P(("dp", "expert"), "mp"),
            P(("dp", "expert"), None),
            P(("dp", "expert")),
            P(),
            P(None, ("expert", "mp")),
            P(("expert", "mp"), None),
        ),
        out_specs=P(("dp", "expert"), "mp"),
        check_vma=False,
    )
```

profile of v0, /device:TPU:0, one launch (start us, length us, event | category | flops | bytes accessed | tf_op | source)
XLA Modules:
  0.0 125.2 jit_solution(13547881894279892863)
XLA Ops:
  6.5 0.7 convert_reduce_fusion
  7.2 0.1 convolution_convert_fusion.2
  7.4 0.8 select_reduce_fusion.1
  8.2 0.7 add_select_fusion
  8.9 17.6 %all_gather.3 = bf16[128,2048]{1,0:T(8,128)(2,1)S(1)} all-gather(bf16[128,512]{1,0:T(8,128)(2,1)} %param.6), channel_id=1, replica_groups=mesh['dp'=2,'expert'=4,'mp'=4] {'mp'}, dimensions={1}, use_global_device_ids=true | all-gather | bytes 655360 | tf_op jit(solution)/shard_map/all_gather | solution.py:33
  26.5 0.6 convolution_convert_fusion.1
  27.1 22.6 %all_to_all.10 = bf16[4,96,2048]{2,1,0:T(8,128)(2,1)S(1)} all-to-all(bf16[4,96,2048]{2,1,0:T(8,128)(2,1)S(1)} %bitcast.15), channel_id=1, replica_groups=mesh['dp'=2,'expert'=4,'mp'=4] {'expert'}, dimensions={0} | all-to-all | bytes 3145728 | tf_op jit(solution)/shard_map/all_to_all | solution.py:40
  49.7 13.1 %convolution_convert_fusion = bf16[384,2048]{1,0:T(8,128)(2,1)} fusion(bf16[1792,2048]{1,0:T(8,128)(2,1)} %param.11, bf16[384,2048]{1,0:T(8,128)(2,1)S(1)} %bitcast.17, bf16[2048,1792]{1,0:T(8,128)(2,1)} %param.10), kind=kOutput, calls=%fused_computation | convolution fusion | flops 5641371648 | bytes 17825792 | tf_op jit(solution)/shard_map/dot_general | solution.py:52
  62.8 0.0 copy-start
  62.8 3.7 %all-to-all-start.1 = ((bf16[4,96,2048]{2,1,0:T(8,128)(2,1)}), bf16[4,96,2048]{2,1,0:T(8,128)(2,1)S(1)}, u32[]{:S(2)}, u32[]{:S(2)}) async-start(bf16[4,96,2048]{2,1,0:T(8,128)(2,1)} %bitcast.4), calls=%async_computation.1 | async-start | bytes 3145728 | tf_op jit(solution)/shard_map/all_to_all | solution.py:53
  66.5 0.0 reduce-scatter.2.cloned.1.call-start
  66.5 0.0 copy-done
  66.6 0.1 select_reduce_fusion
  66.7 19.8 %all-to-all-done.1 = bf16[4,96,2048]{2,1,0:T(8,128)(2,1)S(1)} async-done(((bf16[4,96,2048]{2,1,0:T(8,128)(2,1)}), bf16[4,96,2048]{2,1,0:T(8,128)(2,1)S(1)}, u32[]{:S(2)}, u32[]{:S(2)}) %all-to-all-start.1) | async-done | bytes 1572896 | tf_op jit(solution)/shard_map/all_to_all | solution.py:53
  86.5 2.0 %fusion.7 = f32[128,2048]{1,0:T(8,128)} fusion(f32[128,384]{1,0:T(8,128)S(1)} %select_reduce_fusion, bf16[384,2048]{1,0:T(8,128)(2,1)S(1)} %bitcast.16), kind=kOutput, calls=%fused_computation.22 | convolution fusion | flops 1207959552 | bytes 2818048 | tf_op jit(solution)/shard_map/dot_general | solution.py:66
  88.5 0.0 reduce-scatter.2.cloned.1.call-update
  88.5 28.3 %reduce-scatter.2.cloned.1.call-done = f32[128,512]{1,0:T(8,128)} async-done(((f32[128,2048]{1,0:T(8,128)}), f32[128,512]{1,0:T(8,128)}) %reduce-scatter.2.cloned.1.call-update) | async-done | bytes 262160 | tf_op jit(solution)/shard_map/reduce_scatter | solution.py:69
  116.7 1.6 %convert_element_type.34 = bf16[128,512]{1,0:T(8,128)(2,1)} convert(f32[128,512]{1,0:T(8,128)} %reduce-scatter.2.cloned.1.call-done) | non-fusion elementwise | flops 65536 | bytes 393216 | tf_op jit(solution)/shard_map/convert_element_type | solution.py:69
  (3 shorter events, 0.1 us)
Async XLA Ops:
  62.8 3.8 %copy-start = (s32[128]{0:T(128)S(1)}, s32[128]{0:T(128)}, u32[]{:S(2)}) copy-start(s32[128]{0:T(128)} %param.8) | copy-start | bytes 1540
  62.8 23.7 %all-to-all-start.1 = ((bf16[4,96,2048]{2,1,0:T(8,128)(2,1)}), bf16[4,96,2048]{2,1,0:T(8,128)(2,1)S(1)}, u32[]{:S(2)}, u32[]{:S(2)}) async-start(bf16[4,96,2048]{2,1,0:T(8,128)(2,1)} %bitcast.4), calls=%async_computation.1 | async-start | bytes 3145728 | tf_op jit(solution)/shard_map/all_to_all | solution.py:53
  66.5 50.3 %reduce-scatter.2.cloned.1.call-start = ((), (), s32[]{:S(2)}) async-start(), calls=%async_computation.3 | async-start | bytes 1310720 | tf_op jit(solution)/shard_map/reduce_scatter | solution.py:69
Sparse Core Ops, SparseCore 0:
  88.6 28.0 reduce-scatter.1
where the time goes:
time: 126 us; the launch traced here: 125 us
  waiting for transfers between devices  48.1 us (38%)
  blocking collectives  40.2 us (32%)
  matrix products  15.7 us (12%)
  between operations  13.5 us (11%)
  other arithmetic  4.04 us (3%)
  starting transfers between devices  3.73 us (3%)
    reduce_scatter x1, waiting for transfers between devices, per_device(): lax.psum_scatter(mixed, 'mp', scatter_dimension=1, tiled=True)  28.3 us
    all_to_all x1, blocking collectives, per_device(): lax.all_to_all(copies.reshape(expert_count * group_size, slot_count, widt...  22.6 us
    all_to_all x1, waiting for transfers between devices, per_device(): lax.all_to_all(partial_value.reshape(source_count, count_here, width), 'e...  19.8 us
    all_gather x1, blocking collectives, per_device(): whole = lax.all_gather(tokens, 'mp', axis=1, tiled=True)  17.6 us
    dot_general x1, matrix products, per_device(): jnp.dot(hidden, w_down, preferred_element_type=jnp.float32)  13.1 us
    all_to_all x1, starting transfers between devices, per_device(): lax.all_to_all(partial_value.reshape(source_count, count_here, width), 'e...  3.69 us
  transfers between devices with their start and end apart: 2, of which 2 were waited for; matrix products, arithmetic and copies ran while one was open for 0% of the time, Pallas kernels for 0%

commit v1 on v0

--- a/solution.py
+++ b/solution.py
@@ -1,10 +1,14 @@
+import functools
+
 import jax
 import jax.numpy as jnp
 from jax import lax
+from jax.experimental import pallas as pl
+from jax.experimental.pallas import tpu as pltpu
 from jax.sharding import PartitionSpec as P
 
 
-def per_device(tokens, routes, gate_num, capacity, w_up, w_down):
+def per_device_collectives(tokens, routes, gate_num, capacity, w_up, w_down):
     token_count = routes.shape[0]
     expert_count = capacity.shape[0]
     group_size = lax.axis_size("expert") // expert_count
@@ -68,6 +72,328 @@
     )
     return lax.psum_scatter(mixed, "mp", scatter_dimension=1, tiled=True).astype(jnp.bfloat16)
 
+MESH = pl.DeviceIdType.MESH
+
+
+def flip(index, bits):
+    result, place = 0, 1
+    while place <= bits:
+        bit = lax.rem(index // place, 2)
+        result = result + place * (lax.rem(bit + 1, 2) if bits & place else bit)
+        place *= 2
+    return result + index // place * place
+
+
+def expert_kernel(
+    pieces,
+    slot_count,
+    tile,
+    tokens_ref,
+    meta_ref,
+    capacity_ref,
+    w_up_ref,
+    w_down_ref,
+    out_ref,
+    up_buf,
+    down_buf,
+    rows_buf,
+    meta_buf,
+    slots_buf,
+    pick_buf,
+    mix_buf,
+    acc_buf,
+    hidden_buf,
+    core_out,
+    core_in,
+    keep_buf,
+    y_out,
+    y_in,
+    z_out,
+    z_in,
+    up_sem,
+    down_sem,
+    meta_send,
+    meta_recv,
+    zs,
+    zr,
+    ys,
+    yr,
+    cs,
+    cr,
+    core_send,
+    core_recv,
+    ysum_send,
+    ysum_recv,
+    zsum_send,
+    zsum_recv,
+):
+    token_count, piece_width = tokens_ref.shape
+    hidden_width = up_buf.shape[1]
+    e = lax.axis_index("expert")
+    m = lax.axis_index("mp")
+    partner = {"expert": flip(e, 1)}
+    across = {"expert": flip(e, 2)}
+    peers = [None] + [{"mp": flip(m, j)} for j in range(1, pieces)]
+
+    up_copies, down_copies = [], []
+    for j in range(pieces):
+        start = pl.multiple_of(flip(m, j) * piece_width, piece_width)
+        up_copies.append(
+            pltpu.make_async_copy(
+                w_up_ref.at[pl.ds(start, piece_width), :], up_buf.at[pl.ds(j * piece_width, piece_width), :], up_sem.at[j]
+            )
+        )
+    for copy in up_copies:
+        copy.start()
+    down_copy = pltpu.make_async_copy(w_down_ref, down_buf, down_sem)
+    down_copy.start()
+
+    barrier = pltpu.get_barrier_semaphore()
+    for device in [partner, across] + peers[1:]:
+        pl.semaphore_signal(barrier, inc=1, device_id=device, device_id_type=MESH)
+    pl.semaphore_wait(barrier, pieces + 1)
+
+    def send(src, dst, send_sem, recv_sem, device):
+        copy = pltpu.make_async_remote_copy(
+            src_ref=src, dst_ref=dst, send_sem=send_sem, recv_sem=recv_sem, device_id=device, device_id_type=MESH
+        )
+        return copy
+
+    meta_copies = [
+        send(meta_ref, meta_buf.at[1], meta_send.at[0], meta_recv.at[0], partner),
+        send(meta_ref, meta_buf.at[2], meta_send.at[1], meta_recv.at[1], across),
+        send(meta_buf.at[2], meta_buf.at[3], meta_send.at[2], meta_recv.at[2], partner),
+    ]
+    z_copies = [None] + [
+        send(tokens_ref, rows_buf.at[0, j], zs.at[j], zr.at[j], peers[j]) for j in range(1, pieces)
+    ]
+
+    def own(j):
+        return tokens_ref if j == 0 else rows_buf.at[0, j]
+
+    y_copies = [send(own(j), rows_buf.at[2, j], ys.at[j], yr.at[j], across) for j in range(pieces)]
+    c_copies = [send(own(j), rows_buf.at[1, j], cs.at[0, j], cr.at[0, j], partner) for j in range(pieces)]
+    d_copies = [
+        send(rows_buf.at[2, j], rows_buf.at[3, j], cs.at[1, j], cr.at[1, j], partner) for j in range(pieces)
+    ]
+    meta_copies[0].start()
+    meta_copies[1].start()
+    for j in range(1, pieces):
+        z_copies[j].start()
+    y_copies[0].start()
+    c_copies[0].start()
+
+    def from_z(j):
+        z_copies[j].wait_recv()
+        y_copies[j].start()
+        c_copies[j].start()
+
+    def from_y(j):
+        y_copies[j].wait_recv()
+        d_copies[j].start()
+
+    def select():
+        meta_copies[0].wait_recv()
+        meta_copies[2].wait_recv()
+        limit = capacity_ref[e].astype(jnp.float32)
+        before = lax.broadcasted_iota(jnp.int32, (token_count, token_count), 0)
+        after = lax.broadcasted_iota(jnp.int32, (token_count, token_count), 1)
+        earlier = jnp.where(before < after, 1.0, 0.0).astype(jnp.bfloat16)
+        slot_ids = lax.broadcasted_iota(jnp.int32, (slot_count, token_count), 0).astype(jnp.float32)
+        for r in range(4):
+            meta = meta_ref[...] if r == 0 else meta_buf[r]
+            first, second, gate = meta[0:1, :], meta[1:2, :], meta[2:3, :]
+            named = jnp.where((first == e) | (second == e), 1.0, 0.0)
+            position = jnp.dot(
+                jnp.broadcast_to(named, (16, token_count)).astype(jnp.bfloat16),
+                earlier,
+                preferred_element_type=jnp.float32,
+            )[0:1, :]
+            slot = jnp.where((named > 0.5) & (position < limit), position, -1.0)
+            share = gate.astype(jnp.float32) / 64.0
+            weight = jnp.where(first == e, share, 1.0 - share)
+            hit = jnp.where(slot_ids == slot, 1.0, 0.0)
+            pick_buf[r] = hit.astype(jnp.bfloat16)
+            mix_buf[r] = (hit * weight).astype(jnp.bfloat16)
+
+    def up_piece(j):
+        c_copies[j].wait_recv()
+        d_copies[j].wait_recv()
+        up_copies[j].wait()
+        for r in range(4):
+            rows = own(j)[...] if r == 0 else rows_buf[r, j]
+            slots_buf[pl.ds(r * slot_count, slot_count), :] = jnp.dot(
+                pick_buf[r], rows, preferred_element_type=jnp.float32
+            ).astype(jnp.bfloat16)
+
+        def column(i, carry):
+            columns = pl.ds(pl.multiple_of(i * tile, tile), tile)
+            value = jnp.dot(
+                slots_buf[...],
+                up_buf[pl.ds(j * piece_width, piece_width), columns],
+                preferred_element_type=jnp.float32,
+            )
+            if j > 0:
+                value = acc_buf[:, columns] + value
+            if j < pieces - 1:
+                acc_buf[:, columns] = value
+            else:
+                hidden_buf[:, columns] = (value / (1.0 + jnp.exp(-value))).astype(jnp.bfloat16)
+            return carry
+
+        lax.fori_loop(0, hidden_width // tile, column, 0)
+
+    meta_copies[1].wait_recv()
+    meta_copies[2].start()
+    select()
+    if pieces > 1:
+        from_z(1)
+    from_y(0)
+    for j in range(pieces):
+        up_piece(j)
+        if j + 2 < pieces:
+            from_z(j + 2)
+        if j + 1 < pieces:
+            from_y(j + 1)
+
+    down_copy.wait()
+    core_copies = [
+        send(core_out.at[j], core_in.at[j], core_send.at[j], core_recv.at[j], partner) for j in range(pieces)
+    ]
+    ysum_copies = [send(y_out.at[j], y_in.at[j], ysum_send.at[j], ysum_recv.at[j], across) for j in range(pieces)]
+    zsum_copies = [None] + [
+        send(z_out.at[j], z_in.at[j], zsum_send.at[j], zsum_recv.at[j], peers[j]) for j in range(1, pieces)
+    ]
+
+    def down_piece(j):
+        base = flip(m, j) * piece_width
+
+        def column(i, carry):
+            local = pl.ds(pl.multiple_of(i * tile, tile), tile)
+            columns = pl.ds(pl.multiple_of(base + i * tile, tile), tile)
+            partial = jnp.dot(
+                hidden_buf[...], down_buf[:, columns], preferred_element_type=jnp.float32
+            ).astype(jnp.bfloat16)
+            for r in (1, 3, 0, 2):
+                mixed = lax.dot_general(
+                    mix_buf[r],
+                    partial[r * slot_count : (r + 1) * slot_count, :],
+                    (((0,), (0,)), ((), ())),
+                    preferred_element_type=jnp.float32,
+                )
+                if r % 2 == 1:
+                    core_out[j, r // 2, :, local] = mixed.astype(jnp.bfloat16)
+                else:
+                    keep_buf[j, r // 2, :, local] = mixed
+            return carry
+
+        lax.fori_loop(0, piece_width // tile, column, 0)
+        core_copies[j].start()
+
+    def to_y(j):
+        core_copies[j].wait_recv()
+        y_out[j] = (keep_buf[j, 1] + core_in[j, 1].astype(jnp.float32)).astype(jnp.bfloat16)
+        ysum_copies[j].start()
+
+    def own_sum(j):
+        ysum_copies[j].wait_recv()
+        return keep_buf[j, 0] + core_in[j, 0].astype(jnp.float32) + y_in[j].astype(jnp.float32)
+
+    def to_z(j):
+        z_out[j] = own_sum(j).astype(jnp.bfloat16)
+        zsum_copies[j].start()
+
+    order = list(range(pieces - 1, -1, -1))
+    for step in range(pieces + 2):
+        if step < pieces:
+            down_piece(order[step])
+        if 1 <= step <= pieces:
+            to_y(order[step - 1])
+        if step >= 2 and order[step - 2] > 0:
+            to_z(order[step - 2])
+    total = own_sum(0)
+    for j in range(pieces - 1, 0, -1):
+        zsum_copies[j].wait_recv()
+        total = total + z_in[j].astype(jnp.float32)
+    out_ref[...] = total.astype(jnp.bfloat16)
+    for copy in (
+        meta_copies + z_copies[1:] + y_copies + c_copies + d_copies + core_copies + ysum_copies + zsum_copies[1:]
+    ):
+        copy.wait_send()
+
+
+def per_device_kernel(tokens, routes, gate_num, capacity, w_up, w_down):
+    token_count, piece_width = tokens.shape
+    pieces = lax.axis_size("mp")
+    expert_count = capacity.shape[0]
+    slot_count = min(token_count, 3 * token_count // expert_count)
+    width, hidden_width = w_up.shape
+    row_count = expert_count * slot_count
+    tile = min(256, piece_width)
+    meta = jnp.concatenate(
+        [routes.T, gate_num[None, :], jnp.zeros((5, token_count), jnp.int32)], axis=0
+    )
+    bf16, f32 = jnp.bfloat16, jnp.float32
+    sem = pltpu.SemaphoreType.DMA
+    block = (token_count, piece_width)
+    return pl.pallas_call(
+        functools.partial(expert_kernel, pieces, slot_count, tile),
+        out_shape=jax.ShapeDtypeStruct(block, bf16),
+        in_specs=[
+            pl.BlockSpec(memory_space=pltpu.VMEM),
+            pl.BlockSpec(memory_space=pltpu.VMEM),
+            pl.BlockSpec(memory_space=pltpu.SMEM),
+            pl.BlockSpec(memory_space=pl.ANY),
+            pl.BlockSpec(memory_space=pl.ANY),
+        ],
+        out_specs=pl.BlockSpec(memory_space=pltpu.VMEM),
+        scratch_shapes=[
+            pltpu.VMEM((width, hidden_width), bf16),
+            pltpu.VMEM((hidden_width, width), bf16),
+            pltpu.VMEM((4, pieces) + block, bf16),
+            pltpu.VMEM((4, 8, token_count), jnp.int32),
+            pltpu.VMEM((row_count, piece_width), bf16),
+            pltpu.VMEM((4, slot_count, token_count), bf16),
+            pltpu.VMEM((4, slot_count, token_count), bf16),
+            pltpu.VMEM((row_count, hidden_width), f32),
+            pltpu.VMEM((row_count, hidden_width), bf16),
+            pltpu.VMEM((pieces, 2) + block, bf16),
+            pltpu.VMEM((pieces, 2) + block, bf16),
+            pltpu.VMEM((pieces, 2) + block, f32),
+            pltpu.VMEM((pieces,) + block, bf16),
+            pltpu.VMEM((pieces,) + block, bf16),
+            pltpu.VMEM((pieces,) + block, bf16),
+            pltpu.VMEM((pieces,) + block, bf16),
+            sem((pieces,)),
+            sem,
+            sem((3,)),
+            sem((3,)),
+            sem((pieces,)),
+            sem((pieces,)),
+            sem((pieces,)),
+            sem((pieces,)),
+            sem((2, pieces)),
+            sem((2, pieces)),
+            sem((pieces,)),
+            sem((pieces,)),
+            sem((pieces,)),
+            sem((pieces,)),
+            sem((pieces,)),
+            sem((pieces,)),
+        ],
+        compiler_params=pltpu.CompilerParams(collective_id=0, has_side_effects=True),
+    )(tokens, meta, capacity, w_up, w_down)
+
+
+def per_device(tokens, routes, gate_num, capacity, w_up, w_down):
+    experts, pieces = lax.axis_size("expert"), lax.axis_size("mp")
+    weight_bytes = 2 * w_up.size * w_up.dtype.itemsize
+    fits = experts == 4 and capacity.shape[0] == 4 and pieces & (pieces - 1) == 0
+    fits = fits and weight_bytes <= 24 << 20 and tokens.shape[0] == 128
+    fits = fits and tokens.shape[1] % 256 == 0 and w_up.shape[1] % 256 == 0
+    body = per_device_kernel if fits else per_device_collectives
+    return body(tokens, routes, gate_num, capacity, w_up, w_down)
+
 
 def solution(mesh):
     return jax.shard_map(

time: 126 us -> 53.4 us (0.42)
  Pallas kernels: 0 us -> 50.2 us
  waiting for transfers between devices: 48.1 us -> 0 us
  blocking collectives: 40.2 us -> 0 us
  matrix products: 15.7 us -> 0 us
  between operations: 13.5 us -> 0.01 us
  starting transfers between devices: 3.73 us -> 0 us
  other arithmetic: 4.04 us -> 1.36 us
  local copies, waits for them, and re-layouts: 0.01 us -> 1.65 us
    pallas_call x0 -> x1, Pallas kernels: none -> 50.2 us  [per_device_kernel(): pl.pallas_call(functools.partial(expert_kernel, pieces, slot_count, tile)...]
    reduce_scatter x1 -> x0, waiting for transfers between devices: 28.3 us -> none  [per_device(): lax.psum_scatter(mixed, 'mp', scatter_dimension=1, tiled=True)]
    all_to_all x1 -> x0, blocking collectives: 22.6 us -> none  [per_device(): lax.all_to_all(copies.reshape(expert_count * group_size, slot_count, widt...]
    all_to_all x1 -> x0, waiting for transfers between devices: 19.8 us -> none  [per_device(): lax.all_to_all(partial_value.reshape(source_count, count_here, width), 'e...]
    all_gather x1 -> x0, blocking collectives: 17.6 us -> none  [per_device(): whole = lax.all_gather(tokens, 'mp', axis=1, tiled=True)]
    dot_general x4 -> x0, matrix products: 15.7 us -> none  [the longest x1 13.1 us: per_device(): jnp.dot(hidden, w_down, preferred_element_type=jnp.float32)]
    all_to_all x1 -> x0, starting transfers between devices: 3.69 us -> none  [per_device(): lax.all_to_all(partial_value.reshape(source_count, count_here, width), 'e...]
    reduce_sum x3 -> x0, other arithmetic: 1.67 us -> none  [the longest x1 0.85 us: per_device(): route_cap = jnp.sum(jnp.where(matches, capacity[None, None, :], 0), axis=2)]
  transfers between devices with their start and end apart: 2 -> 0, of which waited for: 2 -> 0; matrix products, arithmetic and copies ran while one was open for 0% -> 0% of each run, Pallas kernels for 0% -> 0%
where the time goes in v1:
time: 53.4 us; the launch traced here: 53.3 us
  Pallas kernels  50.2 us (94%)
  local copies, waits for them, and re-layouts  1.65 us (3%)
  other arithmetic  1.36 us (3%)
    pallas_call x1, Pallas kernels, per_device_kernel(): pl.pallas_call(functools.partial(expert_kernel, pieces, slot_count, tile)...  50.2 us
    unnamed x1, local copies, waits for them, and re-layouts  1.57 us
    concatenate x1, other arithmetic, per_device_kernel(): jnp.concatenate([routes.T, gate_num[None, :], jnp.zeros((5, token_count),...  1.36 us

profile of v1, /device:TPU:0, one launch (start us, length us, event | category | flops | bytes accessed | tf_op | source)
XLA Modules:
  0.0 53.3 jit_solution(9406494708084134786)
XLA Ops:
  0.0 0.1 pad.2.clone
  0.1 1.4 %add_add_fusion.meta_ref = s32[8,128]{1,0:T(8,128)} fusion(s32[1,128]{1,0:T(1,128)} %bitcast.3, s32[2,128]{1,0:T(2,128)} %bitcast.2, s32[8]{0:T(128)S(1)} %pad.2.clone), kind=kLoop, calls=%fused_computation | loop fusion | flops 2048 | bytes 5664 | tf_op jit(solution)/shard_map/concatenate | solution.py:333
  1.4 50.2 %shard_map.64 = bf16[128,512]{1,0:T(8,128)(2,1)} custom-call(bf16[128,512]{1,0:T(8,128)(2,1)} %tokens_ref.1, s32[8,128]{1,0:T(8,128)} %add_add_fusion.meta_ref, s32[4]{0:T(128)} %capacity_ref.1, bf16[2048,1792]{1,0:T(8,128)(2,1)} %w_up_ref.1, bf16[1792,2048]{1,0:T(8,128)(2,1)} %w_down_ref.1), custom_call_target="tpu_custom_call" | custom-call | tf_op jit(solution)/shard_map/pallas_call | solution.py:339
  51.7 1.6 %copy.8 = bf16[128,512]{1,0:T(8,128)(2,1)} copy(bf16[128,512]{1,0:T(8,128)(2,1)} %shard_map.64) | data formatting | bytes 262144
  (1 shorter events, 0.0 us)

commit v2 on v0

--- a/solution.py
+++ b/solution.py
@@ -1,10 +1,14 @@
+import functools
+
 import jax
 import jax.numpy as jnp
 from jax import lax
+from jax.experimental import pallas as pl
+from jax.experimental.pallas import tpu as pltpu
 from jax.sharding import PartitionSpec as P
 
 
-def per_device(tokens, routes, gate_num, capacity, w_up, w_down):
+def per_device_collectives(tokens, routes, gate_num, capacity, w_up, w_down):
     token_count = routes.shape[0]
     expert_count = capacity.shape[0]
     group_size = lax.axis_size("expert") // expert_count
@@ -68,6 +72,415 @@
     )
     return lax.psum_scatter(mixed, "mp", scatter_dimension=1, tiled=True).astype(jnp.bfloat16)
 
+MESH = pl.DeviceIdType.MESH
+SLOTS = 4
+
+
+def expert_kernel(
+    slot_count,
+    tile,
+    tokens_ref,
+    routes_ref,
+    gate_ref,
+    capacity_ref,
+    w_up_ref,
+    w_down_ref,
+    out_ref,
+    up_buf,
+    down_buf,
+    rows_buf,
+    routes_buf,
+    gate_buf,
+    slots_buf,
+    pick_buf,
+    mix_buf,
+    acc_buf,
+    hidden_buf,
+    core_out,
+    core_in,
+    keep_buf,
+    y_out,
+    y_in,
+    z_out,
+    z_in,
+    up_sem,
+    down_sem,
+    meta_send,
+    meta_recv,
+    zs,
+    zr,
+    ys,
+    yr,
+    cs,
+    cr,
+    core_send,
+    core_recv,
+    ysum_send,
+    ysum_recv,
+    zsum_send,
+    zsum_recv,
+):
+    token_count, piece_width = tokens_ref.shape
+    hidden_width = up_buf.shape[1]
+    half_rows, half_cols = token_count // 2, piece_width // 2
+    f32, bf16 = jnp.float32, jnp.bfloat16
+    e = lax.axis_index("expert")
+    m = lax.axis_index("mp")
+    upper = m // 2
+    inner = lax.rem(lax.rem(m, 2) + upper, 2)
+    pair_index = m + 1 - 2 * lax.rem(m, 2)
+    facing_index = 3 - m
+    piece_of = [m, pair_index, 2 - upper, 3 - 3 * upper]
+    partner = {"expert": e + 1 - 2 * lax.rem(e, 2)}
+    across = {"expert": lax.rem(e + 2, 4)}
+    pair, facing = {"mp": pair_index}, {"mp": facing_index}
+    onward = {"mp": inner * facing_index + (1 - inner) * pair_index}
+    is_inner, is_end = inner == 1, inner == 0
+    halves = range(2)
+
+    up_copies = []
+    for s in range(SLOTS):
+        start = pl.multiple_of(piece_of[s] * piece_width, piece_width)
+        up_copies.append(
+            pltpu.make_async_copy(
+                w_up_ref.at[pl.ds(start, piece_width), :],
+                up_buf.at[pl.ds(s * piece_width, piece_width), :],
+                up_sem.at[s],
+            )
+        )
+    for copy in up_copies:
+        copy.start()
+    down_copy = pltpu.make_async_copy(w_down_ref, down_buf, down_sem)
+    down_copy.start()
+
+    barrier = pltpu.get_barrier_semaphore()
+    for device in (partner, across, pair):
+        pl.semaphore_signal(barrier, inc=1, device_id=device, device_id_type=MESH)
+
+    @pl.when(is_inner)
+    def _():
+        pl.semaphore_signal(barrier, inc=1, device_id=facing, device_id_type=MESH)
+
+    pl.semaphore_wait(barrier, 3 + inner)
+
+    def send(src, dst, send_sem, recv_sem, device):
+        return pltpu.make_async_remote_copy(
+            src_ref=src, dst_ref=dst, send_sem=send_sem, recv_sem=recv_sem, device_id=device, device_id_type=MESH
+        )
+
+    def own(s, h):
+        rows = pl.ds(h * half_rows, half_rows)
+        return tokens_ref.at[rows, :] if s == 0 else rows_buf.at[0, s, rows, :]
+
+    def slot(r, s, h):
+        return rows_buf.at[r, s, pl.ds(h * half_rows, half_rows), :]
+
+    meta_copies = []
+    for i, (ref, buf) in enumerate(((routes_ref, routes_buf), (gate_ref, gate_buf))):
+        meta_copies.append(
+            (
+                send(ref, buf.at[1], meta_send.at[i, 0], meta_recv.at[i, 0], partner),
+                send(ref, buf.at[2], meta_send.at[i, 1], meta_recv.at[i, 1], across),
+                send(buf.at[2], buf.at[3], meta_send.at[i, 2], meta_recv.at[i, 2], partner),
+            )
+        )
+    to_pair = [send(own(0, h), slot(0, 1, h), zs.at[0, h], zr.at[1, h], pair) for h in halves]
+    relays = {}
+    relays[0] = [send(own(0, h), slot(0, 2, h), zs.at[1, h], zr.at[2, h], facing) for h in halves]
+    relays[1] = [send(slot(0, 1, h), slot(0, 3, h), zs.at[2, h], zr.at[3, h], facing) for h in halves]
+    relays[2] = [send(slot(0, 2, h), slot(0, 2, h), zs.at[3, h], zr.at[2, h], pair) for h in halves]
+    relays[3] = [send(slot(0, 3, h), slot(0, 3, h), zs.at[4, h], zr.at[3, h], pair) for h in halves]
+    z_arrivals = {1: to_pair, 2: relays[0], 3: relays[1]}
+
+    y_copies = [[send(own(s, h), slot(2, s, h), ys.at[s, h], yr.at[s, h], across) for h in halves] for s in range(SLOTS)]
+    c_copies = [
+        [send(own(s, h), slot(1, s, h), cs.at[0, s, h], cr.at[0, s, h], partner) for h in halves] for s in range(SLOTS)
+    ]
+    d_copies = [
+        [send(slot(2, s, h), slot(3, s, h), cs.at[1, s, h], cr.at[1, s, h], partner) for h in halves]
+        for s in range(SLOTS)
+    ]
+
+    def spread(s, h):
+        if s > 0:
+            z_arrivals[s][h].wait_recv()
+
+        @pl.when(is_inner)
+        def _():
+            relays[s][h].start()
+
+        y_copies[s][h].start()
+        c_copies[s][h].start()
+
+    def from_y(s, h):
+        y_copies[s][h].wait_recv()
+        d_copies[s][h].start()
+
+    def select():
+        for copies in meta_copies:
+            copies[0].wait_recv()
+            copies[2].wait_recv()
+        limit = capacity_ref[e].astype(f32)
+        before = lax.broadcasted_iota(jnp.int32, (token_count, token_count), 0)
+        after = lax.broadcasted_iota(jnp.int32, (token_count, token_count), 1)
+        earlier = jnp.where(before < after, 1.0, 0.0).astype(bf16)
+        slot_ids = lax.broadcasted_iota(jnp.int32, (slot_count, token_count), 0).astype(f32)
+        for r in range(4):
+            routes = routes_ref[...] if r == 0 else routes_buf[r]
+            gate = gate_ref[...] if r == 0 else gate_buf[r]
+            first, second = routes[0:1, :], routes[1:2, :]
+            named = jnp.where((first == e) | (second == e), 1.0, 0.0)
+            position = jnp.dot(
+                jnp.broadcast_to(named, (16, token_count)).astype(bf16), earlier, preferred_element_type=f32
+            )[0:1, :]
+            place = jnp.where((named > 0.5) & (position < limit), position, -1.0)
+            share = gate.astype(f32) / 64.0
+            weight = jnp.where(first == e, share, 1.0 - share)
+            hit = jnp.where(slot_ids == place, 1.0, 0.0)
+            pick_buf[r] = hit.astype(bf16)
+            mix_buf[r] = (hit * weight).astype(bf16)
+
+    def up_piece(s):
+        for h in halves:
+            c_copies[s][h].wait_recv()
+            d_copies[s][h].wait_recv()
+        up_copies[s].wait()
+        for r in range(4):
+            rows = tokens_ref[...] if r == 0 and s == 0 else rows_buf[r, s]
+            slots_buf[pl.ds(r * slot_count, slot_count), :] = jnp.dot(
+                pick_buf[r], rows, preferred_element_type=f32
+            ).astype(bf16)
+
+        def column(i, carry):
+            columns = pl.ds(pl.multiple_of(i * tile, tile), tile)
+            value = jnp.dot(
+                slots_buf[...], up_buf[pl.ds(s * piece_width, piece_width), columns], preferred_element_type=f32
+            )
+            if s > 0:
+                value = acc_buf[:, columns] + value
+            if s < SLOTS - 1:
+                acc_buf[:, columns] = value
+            else:
+                hidden_buf[:, columns] = (value / (1.0 + jnp.exp(-value))).astype(bf16)
+            return carry
+
+        lax.fori_loop(0, hidden_width // tile, column, 0)
+
+    for copies in meta_copies:
+        copies[0].start()
+        copies[1].start()
+    for h in halves:
+        to_pair[h].start()
+        spread(0, h)
+    for copies in meta_copies:
+        copies[1].wait_recv()
+        copies[2].start()
+    select()
+    for h in halves:
+        spread(1, h)
+        from_y(0, h)
+    for h in halves:
+        spread(2, h)
+
+    @pl.when(is_inner)
+    def _():
+        for h in halves:
+            z_arrivals[3][h].wait_recv()
+            relays[3][h].start()
+            y_copies[3][h].start()
+            c_copies[3][h].start()
+
+    up_piece(0)
+
+    @pl.when(is_end)
+    def _():
+        for h in halves:
+            z_arrivals[3][h].wait_recv()
+            y_copies[3][h].start()
+            c_copies[3][h].start()
+
+    for h in halves:
+        from_y(1, h)
+    up_piece(1)
+    for h in halves:
+        from_y(2, h)
+    from_y(3, 0)
+    up_piece(2)
+    from_y(3, 1)
+    up_piece(3)
+
+    down_copy.wait()
+
+    core_copies = [
+        [send(core_out.at[s, h], core_in.at[s, h], core_send.at[s, h], core_recv.at[s, h], partner) for h in halves]
+        for s in range(SLOTS)
+    ]
+    ysum_copies = [
+        [send(y_out.at[s, h], y_in.at[s, h], ysum_send.at[s, h], ysum_recv.at[s, h], across) for h in halves]
+        for s in range(SLOTS)
+    ]
+    zsum_copies = {}
+    for s in (1, 2, 3):
+        place, device = (2, pair) if s == 1 else (3 - s + 3 * inner, onward)
+        zsum_copies[s] = [
+            send(z_out.at[s, h], z_in.at[place, h], zsum_send.at[s, h], zsum_recv.at[place, h], device) for h in halves
+        ]
+
+    def z_arrived(place, h):
+        send(z_out.at[1, h], z_in.at[place, h], zsum_send.at[1, h], zsum_recv.at[place, h], pair).wait_recv()
+        return z_in[place, h].astype(f32)
+
+    def down_piece(s, h):
+        columns = pl.ds(pl.multiple_of(piece_of[s] * piece_width + h * half_cols, half_cols), half_cols)
+        partial = jnp.dot(hidden_buf[...], down_buf[:, columns], preferred_element_type=f32).astype(bf16)
+        for r in (1, 3, 0, 2):
+            mixed = lax.dot_general(
+                mix_buf[r],
+                partial[r * slot_count : (r + 1) * slot_count, :],
+                (((0,), (0,)), ((), ())),
+                preferred_element_type=f32,
+            )
+            if r % 2 == 1:
+                core_out[s, h, r // 2] = mixed.astype(bf16)
+            else:
+                keep_buf[s, h, r // 2] = mixed
+        core_copies[s][h].start()
+
+    def to_y(s, h):
+        core_copies[s][h].wait_recv()
+        y_out[s, h] = (keep_buf[s, h, 1] + core_in[s, h, 1].astype(f32)).astype(bf16)
+        ysum_copies[s][h].start()
+
+    def own_sum(s, h):
+        ysum_copies[s][h].wait_recv()
+        return keep_buf[s, h, 0] + core_in[s, h, 0].astype(f32) + y_in[s, h].astype(f32)
+
+    def end_to_z(s, h):
+        @pl.when(is_end)
+        def _():
+            z_out[s, h] = own_sum(s, h).astype(bf16)
+            zsum_copies[s][h].start()
+
+    def inner_to_z(s, h):
+        @pl.when(is_inner)
+        def _():
+            place = 3 if s == 1 else 3 - s
+            z_out[s, h] = (own_sum(s, h) + z_arrived(place, h)).astype(bf16)
+            zsum_copies[s][h].start()
+
+    order = [(s, h) for s in (3, 2, 1, 0) for h in halves]
+    for step in range(len(order) + 1):
+        if step < len(order):
+            down_piece(*order[step])
+        if step >= 1:
+            to_y(*order[step - 1])
+        if 5 <= step < 9:
+            end_to_z(*order[step - 5])
+    for step in range(4):
+        inner_to_z(*order[step])
+    for h in halves:
+        end_to_z(1, h)
+    for h in halves:
+        inner_to_z(1, h)
+    for h in halves:
+        total = own_sum(0, h) + z_arrived(2, h)
+        keep_buf[0, h, 0] = total
+
+        @pl.when(is_inner)
+        def _():
+            keep_buf[0, h, 0] = keep_buf[0, h, 0] + z_arrived(4, h)
+
+        out_ref[:, h * half_cols : (h + 1) * half_cols] = keep_buf[0, h, 0].astype(bf16)
+
+    for copies in meta_copies:
+        for copy in copies:
+            copy.wait_send()
+    for h in halves:
+        to_pair[h].wait_send()
+        for s in range(SLOTS):
+            y_copies[s][h].wait_send()
+            c_copies[s][h].wait_send()
+            d_copies[s][h].wait_send()
+            core_copies[s][h].wait_send()
+            ysum_copies[s][h].wait_send()
+            if s > 0:
+                zsum_copies[s][h].wait_send()
+
+    @pl.when(is_inner)
+    def _():
+        for s in range(SLOTS):
+            for h in halves:
+                relays[s][h].wait_send()
+
+
+def per_device_kernel(tokens, routes, gate_num, capacity, w_up, w_down):
+    token_count, piece_width = tokens.shape
+    expert_count = capacity.shape[0]
+    slot_count = min(token_count, 3 * token_count // expert_count)
+    width, hidden_width = w_up.shape
+    row_count = expert_count * slot_count
+    bf16, f32 = jnp.bfloat16, jnp.float32
+    sem = pltpu.SemaphoreType.DMA
+    block = (token_count, piece_width)
+    half = (token_count, piece_width // 2)
+    in_vmem = pl.BlockSpec(memory_space=pltpu.VMEM)
+    return pl.pallas_call(
+        functools.partial(expert_kernel, slot_count, 256),
+        out_shape=jax.ShapeDtypeStruct(block, bf16),
+        in_specs=[in_vmem] * 3
+        + [pl.BlockSpec(memory_space=pltpu.SMEM)]
+        + [pl.BlockSpec(memory_space=pl.ANY)] * 2,
+        out_specs=in_vmem,
+        scratch_shapes=[
+            pltpu.VMEM((width, hidden_width), bf16),
+            pltpu.VMEM((hidden_width, width), bf16),
+            pltpu.VMEM((4, SLOTS) + block, bf16),
+            pltpu.VMEM((4, 2, token_count), jnp.int32),
+            pltpu.VMEM((4, 1, token_count), jnp.int32),
+            pltpu.VMEM((row_count, piece_width), bf16),
+            pltpu.VMEM((4, slot_count, token_count), bf16),
+            pltpu.VMEM((4, slot_count, token_count), bf16),
+            pltpu.VMEM((row_count, hidden_width), f32),
+            pltpu.VMEM((row_count, hidden_width), bf16),
+            pltpu.VMEM((SLOTS, 2, 2) + half, bf16),
+            pltpu.VMEM((SLOTS, 2, 2) + half, bf16),
+            pltpu.VMEM((SLOTS, 2, 2) + half, f32),
+            pltpu.VMEM((SLOTS, 2) + half, bf16),
+            pltpu.VMEM((SLOTS, 2) + half, bf16),
+            pltpu.VMEM((SLOTS, 2) + half, bf16),
+            pltpu.VMEM((5, 2) + half, bf16),
+            sem((SLOTS,)),
+            sem,
+            sem((2, 3)),
+            sem((2, 3)),
+            sem((5, 2)),
+            sem((SLOTS, 2)),
+            sem((SLOTS, 2)),
+            sem((SLOTS, 2)),
+            sem((2, SLOTS, 2)),
+            sem((2, SLOTS, 2)),
+            sem((SLOTS, 2)),
+            sem((SLOTS, 2)),
+            sem((SLOTS, 2)),
+            sem((SLOTS, 2)),
+            sem((SLOTS, 2)),
+            sem((5, 2)),
+        ],
+        compiler_params=pltpu.CompilerParams(
+            collective_id=0, has_side_effects=True, vmem_limit_bytes=58 << 20
+        ),
+    )(tokens, routes.T, gate_num[None, :], capacity, w_up, w_down)
+
+
+def per_device(tokens, routes, gate_num, capacity, w_up, w_down):
+    experts, pieces = lax.axis_size("expert"), lax.axis_size("mp")
+    weight_bytes = 2 * w_up.size * w_up.dtype.itemsize
+    fits = experts == 4 and capacity.shape[0] == 4 and pieces == SLOTS
+    fits = fits and weight_bytes <= 24 << 20 and tokens.shape[0] == 128
+    fits = fits and tokens.shape[1] % 256 == 0 and w_up.shape[1] % 256 == 0
+    body = per_device_kernel if fits else per_device_collectives
+    return body(tokens, routes, gate_num, capacity, w_up, w_down)
+
 
 def solution(mesh):
     return jax.shard_map(

time: 126 us -> 50.1 us (0.40)
  Pallas kernels: 0 us -> 48.4 us
  waiting for transfers between devices: 48.1 us -> 0 us
  blocking collectives: 40.2 us -> 0 us
  matrix products: 15.7 us -> 0 us
  between operations: 13.5 us -> 0.01 us
  other arithmetic: 4.04 us -> 0 us
  starting transfers between devices: 3.73 us -> 0 us
  local copies, waits for them, and re-layouts: 0.01 us -> 1.57 us
    pallas_call x0 -> x1, Pallas kernels: none -> 48.4 us  [per_device_kernel(): pl.pallas_call(functools.partial(expert_kernel, slot_count, 256), out_sha...]
    reduce_scatter x1 -> x0, waiting for transfers between devices: 28.3 us -> none  [per_device(): lax.psum_scatter(mixed, 'mp', scatter_dimension=1, tiled=True)]
    all_to_all x1 -> x0, blocking collectives: 22.6 us -> none  [per_device(): lax.all_to_all(copies.reshape(expert_count * group_size, slot_count, widt...]
    all_to_all x1 -> x0, waiting for transfers between devices: 19.8 us -> none  [per_device(): lax.all_to_all(partial_value.reshape(source_count, count_here, width), 'e...]
    all_gather x1 -> x0, blocking collectives: 17.6 us -> none  [per_device(): whole = lax.all_gather(tokens, 'mp', axis=1, tiled=True)]
    dot_general x4 -> x0, matrix products: 15.7 us -> none  [the longest x1 13.1 us: per_device(): jnp.dot(hidden, w_down, preferred_element_type=jnp.float32)]
    all_to_all x1 -> x0, starting transfers between devices: 3.69 us -> none  [per_device(): lax.all_to_all(partial_value.reshape(source_count, count_here, width), 'e...]
    reduce_sum x3 -> x0, other arithmetic: 1.67 us -> none  [the longest x1 0.85 us: per_device(): route_cap = jnp.sum(jnp.where(matches, capacity[None, None, :], 0), axis=2)]
  transfers between devices with their start and end apart: 2 -> 0, of which waited for: 2 -> 0; matrix products, arithmetic and copies ran while one was open for 0% -> 0% of each run, Pallas kernels for 0% -> 0%
where the time goes in v2:
time: 50.1 us; the launch traced here: 49.9 us
  Pallas kernels  48.4 us (97%)
  local copies, waits for them, and re-layouts  1.57 us (3%)
    pallas_call x1, Pallas kernels, per_device_kernel(): pl.pallas_call(functools.partial(expert_kernel, slot_count, 256), out_sha...  48.4 us
    unnamed x1, local copies, waits for them, and re-layouts  1.57 us

profile of v2, /device:TPU:0, one launch (start us, length us, event | category | flops | bytes accessed | tf_op | source)
XLA Modules:
  0.0 49.9 jit_solution(17729988139628482308)
XLA Ops:
  0.0 48.4 %shard_map.64 = bf16[128,512]{1,0:T(8,128)(2,1)} custom-call(bf16[128,512]{1,0:T(8,128)(2,1)} %tokens_ref.1, s32[2,128]{1,0:T(2,128)} %bitcast.2, s32[1,128]{1,0:T(1,128)} %bitcast.3, s32[4]{0:T(128)} %capacity_ref.1, bf16[2048,1792]{1,0:T(8,128)(2,1)} %w_up_ref.1, bf16[1792,2048]{1,0:T(8,128)(2,1)} %w_down_ref.1), custom_call_target="tpu_custom_call" | custom-call | tf_op jit(solution)/shard_map/pallas_call | solution.py:427
  48.4 1.6 %copy.8 = bf16[128,512]{1,0:T(8,128)(2,1)} copy(bf16[128,512]{1,0:T(8,128)(2,1)} %shard_map.64) | data formatting | bytes 262144

commit v3 on v2

--- a/solution.py
+++ b/solution.py
@@ -103,6 +103,7 @@
     y_in,
     z_out,
     z_in,
+    own_sem,
     up_sem,
     down_sem,
     meta_send,
@@ -138,6 +139,13 @@
     is_inner, is_end = inner == 1, inner == 0
     halves = range(2)
 
+    own_copies = [
+        pltpu.make_async_copy(tokens_ref, rows_buf.at[0, 0], own_sem.at[0]),
+        pltpu.make_async_copy(routes_ref, routes_buf.at[0], own_sem.at[1]),
+        pltpu.make_async_copy(gate_ref, gate_buf.at[0], own_sem.at[2]),
+    ]
+    for copy in own_copies:
+        copy.start()
     up_copies = []
     for s in range(SLOTS):
         start = pl.multiple_of(piece_of[s] * piece_width, piece_width)
@@ -148,19 +156,20 @@
                 up_sem.at[s],
             )
         )
+    barrier = pltpu.get_barrier_semaphore()
+    for device in (partner, across, pair):
+        pl.semaphore_signal(barrier, inc=1, device_id=device, device_id_type=MESH)
+
+    @pl.when(is_inner)
+    def _():
+        pl.semaphore_signal(barrier, inc=1, device_id=facing, device_id_type=MESH)
+
     for copy in up_copies:
         copy.start()
     down_copy = pltpu.make_async_copy(w_down_ref, down_buf, down_sem)
     down_copy.start()
-
-    barrier = pltpu.get_barrier_semaphore()
-    for device in (partner, across, pair):
-        pl.semaphore_signal(barrier, inc=1, device_id=device, device_id_type=MESH)
-
-    @pl.when(is_inner)
-    def _():
-        pl.semaphore_signal(barrier, inc=1, device_id=facing, device_id_type=MESH)
-
+    for copy in own_copies:
+        copy.wait()
     pl.semaphore_wait(barrier, 3 + inner)
 
     def send(src, dst, send_sem, recv_sem, device):
@@ -168,49 +177,53 @@
             src_ref=src, dst_ref=dst, send_sem=send_sem, recv_sem=recv_sem, device_id=device, device_id_type=MESH
         )
 
-    def own(s, h):
-        rows = pl.ds(h * half_rows, half_rows)
-        return tokens_ref.at[rows, :] if s == 0 else rows_buf.at[0, s, rows, :]
-
     def slot(r, s, h):
         return rows_buf.at[r, s, pl.ds(h * half_rows, half_rows), :]
 
     meta_copies = []
-    for i, (ref, buf) in enumerate(((routes_ref, routes_buf), (gate_ref, gate_buf))):
+    for i, buf in enumerate((routes_buf, gate_buf)):
         meta_copies.append(
             (
-                send(ref, buf.at[1], meta_send.at[i, 0], meta_recv.at[i, 0], partner),
-                send(ref, buf.at[2], meta_send.at[i, 1], meta_recv.at[i, 1], across),
+                send(buf.at[0], buf.at[1], meta_send.at[i, 0], meta_recv.at[i, 0], partner),
+                send(buf.at[0], buf.at[2], meta_send.at[i, 1], meta_recv.at[i, 1], across),
                 send(buf.at[2], buf.at[3], meta_send.at[i, 2], meta_recv.at[i, 2], partner),
             )
         )
-    to_pair = [send(own(0, h), slot(0, 1, h), zs.at[0, h], zr.at[1, h], pair) for h in halves]
+    to_pair = [send(slot(0, 0, h), slot(0, 1, h), zs.at[0, h], zr.at[1, h], pair) for h in halves]
     relays = {}
-    relays[0] = [send(own(0, h), slot(0, 2, h), zs.at[1, h], zr.at[2, h], facing) for h in halves]
+    relays[0] = [send(slot(0, 0, h), slot(0, 2, h), zs.at[1, h], zr.at[2, h], facing) for h in halves]
     relays[1] = [send(slot(0, 1, h), slot(0, 3, h), zs.at[2, h], zr.at[3, h], facing) for h in halves]
     relays[2] = [send(slot(0, 2, h), slot(0, 2, h), zs.at[3, h], zr.at[2, h], pair) for h in halves]
     relays[3] = [send(slot(0, 3, h), slot(0, 3, h), zs.at[4, h], zr.at[3, h], pair) for h in halves]
     z_arrivals = {1: to_pair, 2: relays[0], 3: relays[1]}
 
-    y_copies = [[send(own(s, h), slot(2, s, h), ys.at[s, h], yr.at[s, h], across) for h in halves] for s in range(SLOTS)]
+    y_copies = [[send(slot(0, s, h), slot(2, s, h), ys.at[s, h], yr.at[s, h], across) for h in halves] for s in range(SLOTS)]
     c_copies = [
-        [send(own(s, h), slot(1, s, h), cs.at[0, s, h], cr.at[0, s, h], partner) for h in halves] for s in range(SLOTS)
+        [send(slot(0, s, h), slot(1, s, h), cs.at[0, s, h], cr.at[0, s, h], partner) for h in halves] for s in range(SLOTS)
     ]
     d_copies = [
         [send(slot(2, s, h), slot(3, s, h), cs.at[1, s, h], cr.at[1, s, h], partner) for h in halves]
         for s in range(SLOTS)
     ]
 
-    def spread(s, h):
+    def spread(s, h, relay):
         if s > 0:
             z_arrivals[s][h].wait_recv()
-
+        if relay:
+            relays[s][h].start()
+        y_copies[s][h].start()
+        c_copies[s][h].start()
+
+    def by_role(inner_step, end_step):
         @pl.when(is_inner)
         def _():
-            relays[s][h].start()
-
-        y_copies[s][h].start()
-        c_copies[s][h].start()
+            for s, h in inner_step:
+                spread(s, h, True)
+
+        @pl.when(is_end)
+        def _():
+            for s, h in end_step:
+                spread(s, h, False)
 
     def from_y(s, h):
         y_copies[s][h].wait_recv()
@@ -226,8 +239,8 @@
         earlier = jnp.where(before < after, 1.0, 0.0).astype(bf16)
         slot_ids = lax.broadcasted_iota(jnp.int32, (slot_count, token_count), 0).astype(f32)
         for r in range(4):
-            routes = routes_ref[...] if r == 0 else routes_buf[r]
-            gate = gate_ref[...] if r == 0 else gate_buf[r]
+            routes = routes_buf[r]
+            gate = gate_buf[r]
             first, second = routes[0:1, :], routes[1:2, :]
             named = jnp.where((first == e) | (second == e), 1.0, 0.0)
             position = jnp.dot(
@@ -240,17 +253,19 @@
             pick_buf[r] = hit.astype(bf16)
             mix_buf[r] = (hit * weight).astype(bf16)
 
-    def up_piece(s):
-        for h in halves:
-            c_copies[s][h].wait_recv()
-            d_copies[s][h].wait_recv()
+    def up_rows(s):
+        for r in range(4):
+            for h in halves:
+                if r == 1:
+                    c_copies[s][h].wait_recv()
+                if r == 3:
+                    d_copies[s][h].wait_recv()
+            slots_buf[pl.ds(r * slot_count, slot_count), :] = jnp.dot(
+                pick_buf[r], rows_buf[r, s], preferred_element_type=f32
+            ).astype(bf16)
         up_copies[s].wait()
-        for r in range(4):
-            rows = tokens_ref[...] if r == 0 and s == 0 else rows_buf[r, s]
-            slots_buf[pl.ds(r * slot_count, slot_count), :] = jnp.dot(
-                pick_buf[r], rows, preferred_element_type=f32
-            ).astype(bf16)
-
+
+    def up_columns(s, start, end):
         def column(i, carry):
             columns = pl.ds(pl.multiple_of(i * tile, tile), tile)
             value = jnp.dot(
@@ -264,50 +279,45 @@
                 hidden_buf[:, columns] = (value / (1.0 + jnp.exp(-value))).astype(bf16)
             return carry
 
-        lax.fori_loop(0, hidden_width // tile, column, 0)
-
+        lax.fori_loop(start, end, column, 0)
+
+    tiles = hidden_width // tile
+    third, half_way = tiles // 3, tiles // 2
+    for h in halves:
+        to_pair[h].start()
+        by_role([(0, h)], [(0, h)])
     for copies in meta_copies:
         copies[0].start()
         copies[1].start()
-    for h in halves:
-        to_pair[h].start()
-        spread(0, h)
     for copies in meta_copies:
         copies[1].wait_recv()
         copies[2].start()
     select()
     for h in halves:
-        spread(1, h)
+        by_role([(1, h), (2, h)], [(1, h)])
         from_y(0, h)
-    for h in halves:
-        spread(2, h)
-
-    @pl.when(is_inner)
-    def _():
-        for h in halves:
-            z_arrivals[3][h].wait_recv()
-            relays[3][h].start()
-            y_copies[3][h].start()
-            c_copies[3][h].start()
-
-    up_piece(0)
-
-    @pl.when(is_end)
-    def _():
-        for h in halves:
-            z_arrivals[3][h].wait_recv()
-            y_copies[3][h].start()
-            c_copies[3][h].start()
-
-    for h in halves:
-        from_y(1, h)
-    up_piece(1)
-    for h in halves:
-        from_y(2, h)
+    up_rows(0)
+    up_columns(0, 0, third)
+    by_role([(3, 0)], [(2, 0)])
+    up_columns(0, third, 2 * third)
+    by_role([(3, 1)], [(2, 1)])
+    from_y(1, 0)
+    from_y(1, 1)
+    up_columns(0, 2 * third, tiles)
+    up_rows(1)
+    up_columns(1, 0, half_way)
+    by_role([], [(3, 0)])
+    up_columns(1, half_way, tiles)
+    by_role([], [(3, 1)])
+    from_y(2, 0)
+    from_y(2, 1)
+    up_rows(2)
+    up_columns(2, 0, half_way)
     from_y(3, 0)
-    up_piece(2)
+    up_columns(2, half_way, tiles)
     from_y(3, 1)
-    up_piece(3)
+    up_rows(3)
+    up_columns(3, 0, tiles)
 
     down_copy.wait()
 
@@ -374,9 +384,11 @@
             down_piece(*order[step])
         if step >= 1:
             to_y(*order[step - 1])
-        if 5 <= step < 9:
-            end_to_z(*order[step - 5])
-    for step in range(4):
+        if 4 <= step < 8:
+            end_to_z(*order[step - 4])
+        if step >= 7:
+            inner_to_z(*order[step - 7])
+    for step in (2, 3):
         inner_to_z(*order[step])
     for h in halves:
         end_to_z(1, h)
@@ -423,13 +435,11 @@
     sem = pltpu.SemaphoreType.DMA
     block = (token_count, piece_width)
     half = (token_count, piece_width // 2)
-    in_vmem = pl.BlockSpec(memory_space=pltpu.VMEM)
+    in_vmem, in_hbm = pl.BlockSpec(memory_space=pltpu.VMEM), pl.BlockSpec(memory_space=pltpu.HBM)
     return pl.pallas_call(
         functools.partial(expert_kernel, slot_count, 256),
         out_shape=jax.ShapeDtypeStruct(block, bf16),
-        in_specs=[in_vmem] * 3
-        + [pl.BlockSpec(memory_space=pltpu.SMEM)]
-        + [pl.BlockSpec(memory_space=pl.ANY)] * 2,
+        in_specs=[in_hbm] * 3 + [pl.BlockSpec(memory_space=pltpu.SMEM)] + [in_hbm] * 2,
         out_specs=in_vmem,
         scratch_shapes=[
             pltpu.VMEM((width, hidden_width), bf16),
@@ -449,6 +459,7 @@
             pltpu.VMEM((SLOTS, 2) + half, bf16),
             pltpu.VMEM((SLOTS, 2) + half, bf16),
             pltpu.VMEM((5, 2) + half, bf16),
+            sem((3,)),
             sem((SLOTS,)),
             sem,
             sem((2, 3)),

time: 50.1 us -> 47.3 us (0.944)
  Pallas kernels: 48.4 us -> 45.6 us
    pallas_call x1, Pallas kernels: 48.4 us -> 45.6 us  [per_device_kernel(): pl.pallas_call(functools.partial(expert_kernel, slot_count, 256), out_sha...]
where the time goes in v3:
time: 47.3 us; the launch traced here: 47.2 us
  Pallas kernels  45.6 us (96%)
  local copies, waits for them, and re-layouts  1.57 us (3%)
    pallas_call x1, Pallas kernels, per_device_kernel(): pl.pallas_call(functools.partial(expert_kernel, slot_count, 256), out_sha...  45.6 us
    unnamed x1, local copies, waits for them, and re-layouts  1.57 us

profile of v3, /device:TPU:0, one launch (start us, length us, event | category | flops | bytes accessed | tf_op | source)
XLA Modules:
  0.0 47.2 jit_solution(9346540080787207662)
XLA Ops:
  0.0 45.6 %shard_map.64 = bf16[128,512]{1,0:T(8,128)(2,1)} custom-call(bf16[128,512]{1,0:T(8,128)(2,1)} %tokens_ref.1, s32[2,128]{1,0:T(2,128)} %bitcast.2, s32[1,128]{1,0:T(1,128)} %bitcast.3, s32[4]{0:T(128)} %capacity_ref.1, bf16[2048,1792]{1,0:T(8,128)(2,1)} %w_up_ref.1, bf16[1792,2048]{1,0:T(8,128)(2,1)} %w_down_ref.1), custom_call_target="tpu_custom_call" | custom-call | tf_op jit(solution)/shard_map/pallas_call | solution.py:439
  45.6 1.6 %copy.8 = bf16[128,512]{1,0:T(8,128)(2,1)} copy(bf16[128,512]{1,0:T(8,128)(2,1)} %shard_map.64) | data formatting | bytes 262144
